TPU v7x, 32 devices: a whole 2x2x4 slice. The times are simulated.
32 devices in a mesh: grp: 2 (over y), fib: 4 (over z), wav: 2 (over x), arm: 2 (over core).
Axes of the slice: x: 2, y: 2, z: 4, core: 2. Of those that a mesh axis runs over, the one named last changes fastest.
Arguments:
- spectra: bfloat16 [32, 2, 2, 128, 256], P(('grp', 'fib'), 'arm', None, None, 'wav'), parts along dimension 0, as said below
- bands: bfloat16 [32, 2, 11, 128, 256], P(('grp', 'fib'), 'arm', None, None, 'wav'), parts along dimension 0, may hold values from 0 to 0.29882812
- coverage: int32 [32, 128], P(('grp', 'fib')), parts along dimension 0, may hold values from 0 to 1, as said below
Outputs:
- flux_coadd: float32 [2, 256, 256], P('arm', ('grp', 'fib'), 'wav'), parts along dimension 1
- ivar_coadd: float32 [2, 256, 256], P('arm', ('grp', 'fib'), 'wav'), parts along dimension 1
- res_coadd: float32 [2, 11, 256, 256], P('arm', None, ('grp', 'fib'), 'wav'), parts along dimension 2
- model: float32 [2, 256, 256], P('arm', ('grp', 'fib'), 'wav'), parts along dimension 1
There are 2 independent parts, one for each index of `grp`. A program takes and returns all parts, laid end to end along the dimension named above; each array names one. Nothing has to cross between parts.
Inputs may be any that keep to these rules, and one draw needn't show every extreme that they name: `spectra`: channel 1 (inverse variance) lies between 0.25 and 4. `coverage`: every fiber is observed by at least one exposure.
All inputs are finite; a program needn't handle non-finite values.
Results may differ from a plain program's by a relative error of at most 0.0003.
Values may be sent and summed in bfloat16 or wider, within the bound.
No kernel may reach another device: no remote copies, remote signals or barrier semaphores. Data moves between devices by JAX's collectives and lax.ppermute only.
A program may use at most 64 MiB of HBM per device.

v0:
```python
import jax
import jax.numpy as jnp
from jax import lax
from jax.sharding import PartitionSpec as P


def padded_2(array, sides, width):
    for axis, dim in sides:
        size, length = (lax.axis_size(axis), array.shape[dim])
        up = [(i, (i + 1) % size) for i in range(size - 1)]
        down = [(j, i) for i, j in up]
        last = lax.slice_in_dim(array, length - width, length, axis=dim)
        leading = lax.slice_in_dim(array, 0, width, axis=dim)
        before = lax.ppermute(last, axis, up)
        after = lax.ppermute(leading, axis, down)
        array = jnp.concatenate([before, array, after], axis=dim)
    return array


def weighted_sums(masked, bands):
    weight = masked[:, :, 1].astype(jnp.float32)
    flux = masked[:, :, 0].astype(jnp.float32)
    ivar_sum = jnp.sum(weight, 0)
    flux_sum = jnp.sum(weight * flux, 0)
    band_sum = jnp.sum(weight[:, :, None] * bands.astype(jnp.float32), 0)
    return jnp.concatenate([ivar_sum[:, None], flux_sum[:, None], band_sum], 1)


def local(spectra, bands, coverage):
    coverage_bf = coverage.astype(jnp.bfloat16)[:, None, :, None]
    masked = jnp.stack([spectra[:, :, 0], spectra[:, :, 1] * coverage_bf], 2)
    totals = lax.psum_scatter(weighted_sums(masked, bands), "fib", scatter_dimension=2, tiled=True)
    ivar_coadd = totals[:, 0]
    flux_coadd = totals[:, 1] / ivar_coadd
    res_coadd = totals[:, 2:] / ivar_coadd[:, None]
    padded = padded_2(flux_coadd, (("wav", 2),), 5)
    width = flux_coadd.shape[2]
    model = res_coadd[:, 0] * padded[:, :, 0:width]
    for band_idx in range(1, res_coadd.shape[1]):
        model = model + res_coadd[:, band_idx] * padded[:, :, band_idx : band_idx + width]
    return (flux_coadd, ivar_coadd, res_coadd, model)


def solution(mesh):
    return jax.shard_map(
        local,
        mesh=mesh,
        in_specs=(
            P(("grp", "fib"), "arm", None, None, "wav"),
            P(("grp", "fib"), "arm", None, None, "wav"),
            P(("grp", "fib"), None),
        ),
        out_specs=(
            P("arm", ("grp", "fib"), "wav"),
            P("arm", ("grp", "fib"), "wav"),
            P("arm", None, ("grp", "fib"), "wav"),
            P("arm", ("grp", "fib"), "wav"),
        ),
        check_vma=False,
    )
```

profile of v0, /device:TPU:0, one launch (start us, length us, event | category | flops | bytes accessed | tf_op | source)
XLA Modules:
  0.0 57.9 jit_solution(12930931305381193282)
XLA Ops:
  7.2 0.0 reduce-scatter.2.cloned.1.call-start
  7.2 0.7 %convert_element_type.36 = bf16[4,128]{1,0:T(4,128)(2,1)S(1)} convert(s32[4,128]{1,0:T(4,128)} %param.5) | non-fusion elementwise | flops 512 | bytes 3072 | tf_op jit(solution)/shard_map/convert_element_type | solution.py:30
  7.9 1.1 %convert_reduce_fusion = (f32[128,128]{1,0:T(8,128)S(1)}, f32[128,128]{1,0:T(8,128)S(1)}) fusion(bf16[4,1,2,128,128]{4,3,2,1,0:T(8,128)(2,1)} %param.3, bf16[4,128]{1,0:T(4,128)(2,1)S(1)} %convert_element_type.36), kind=kLoop, calls=%fused_computation.3 | loop fusion | flops 360448 | bytes 394240 | tf_op jit(solution)/shard_map/reduce_sum | solution.py:23
  9.0 1.0 %fusion.2 = f32[4,128,128]{2,1,0:T(8,128)S(1)} fusion(bf16[4,1,2,128,128]{4,3,2,1,0:T(8,128)(2,1)} %param.3, bf16[4,128]{1,0:T(4,128)(2,1)S(1)} %convert_element_type.36), kind=kLoop, calls=%fused_computation.9 | loop fusion | flops 131072 | bytes 394240 | tf_op jit(solution)/shard_map/mul | solution.py:25
  10.1 1.8 %multiply_reduce_fusion = f32[11,128,128]{2,1,0:T(8,128)S(1)} fusion(bf16[4,1,11,128,128]{4,3,2,1,0:T(8,128)(2,1)} %param.4, f32[4,128,128]{2,1,0:T(8,128)S(1)} %fusion.2), kind=kLoop, calls=%fused_computation | loop fusion | flops 1982464 | bytes 2424832 | tf_op jit(solution)/shard_map/reduce_sum | solution.py:25
  11.8 1.0 %pad_maximum_fusion = f32[1,13,128,128]{3,2,1,0:T(8,128)} fusion(f32[1,11,128,128]{3,2,1,0:T(8,128)S(1)} %bitcast.79, f32[1,1,128,128]{3,2,1,0:T(8,128)S(1)} %bitcast.81, f32[1,1,128,128]{3,2,1,0:T(8,128)S(1)} %bitcast.80), kind=kLoop, calls=%fused_computation.1 | loop fusion | flops 425984 | bytes 1703936 | tf_op jit(solution)/shard_map/concatenate | solution.py:26
  12.8 0.0 reduce-scatter.2.cloned.1.call-update
  12.8 27.1 %reduce-scatter.2.cloned.1.call-done = f32[1,13,32,128]{3,2,1,0:T(8,128)} async-done(((f32[1,13,128,128]{3,2,1,0:T(8,128)}), f32[1,13,32,128]{3,2,1,0:T(8,128)}) %reduce-scatter.2.cloned.1.call-update) | async-done | bytes 213008 | tf_op jit(solution)/shard_map/reduce_scatter | solution.py:32
  39.9 1.3 %fusion.32 = (f32[1,32,128]{2,1,0:T(8,128)S(1)}, f32[1,32,128]{2,1,0:T(8,128)}) fusion(f32[1,13,32,128]{3,2,1,0:T(8,128)} %reduce-scatter.2.cloned.1.call-done), kind=kLoop, calls=%fused_computation.69 | loop fusion | flops 4096 | bytes 65536 | tf_op jit(solution)/shard_map/div | solution.py:34
  41.2 0.0 copy-start.1
  41.2 0.1 fusion.33
  41.3 3.3 %collective-permute-start = (f32[1,32,5]{2,1,0:T(8,128)S(1)}, f32[1,32,5]{2,1,0:T(8,128)S(1)}, u32[]{:S(2)}, u32[]{:S(2)}) collective-permute-start(f32[1,32,5]{2,1,0:T(8,128)S(1)} %get-tuple-element.8), channel_id=1, source_target_pairs={{0,2},{1,3},{4,6},{5,7},{8,10},{9,11},{12,14},{13,15},{16,18},{17,... | collective-permute-start | bytes 1928 | tf_op jit(solution)/shard_map/ppermute | solution.py:14
  44.7 1.3 %collective-permute-start.1 = (f32[1,32,5]{2,1,0:T(8,128)S(1)}, f32[1,32,5]{2,1,0:T(8,128)S(1)}, u32[]{:S(2)}, u32[]{:S(2)}) collective-permute-start(f32[1,32,5]{2,1,0:T(8,128)S(1)} %get-tuple-element.9), channel_id=1, source_target_pairs={{2,0},{3,1},{6,4},{7,5},{10,8},{11,9},{14,12},{15,13},{18,16},{19,... | collective-permute-start | bytes 1928 | tf_op jit(solution)/shard_map/ppermute | solution.py:15
  46.0 0.7 %slice_bitcast_fusion.12 = f32[32,128]{1,0:T(8,128)S(1)} fusion(f32[1,13,32,128]{3,2,1,0:T(8,128)} %reduce-scatter.2.cloned.1.call-done), kind=kLoop, calls=%fused_computation.70 | loop fusion | bytes 32768 | tf_op jit(solution)/shard_map/div | solution.py:35
  46.7 0.9 %slice_divide_fusion = f32[1,11,32,128]{3,2,1,0:T(8,128)S(1)} fusion(f32[1,13,32,128]{3,2,1,0:T(8,128)} %reduce-scatter.2.cloned.1.call-done, f32[32,128]{1,0:T(8,128)S(1)} %slice_bitcast_fusion.12), kind=kLoop, calls=%fused_computation.5 | loop fusion | flops 45056 | bytes 376832 | tf_op jit(solution)/shard_map/div | solution.py:35
  47.6 0.0 copy-start
  47.7 0.0 collective-permute-done
  47.7 2.6 %collective-permute-done.1 = f32[1,32,5]{2,1,0:T(8,128)S(1)} collective-permute-done((f32[1,32,5]{2,1,0:T(8,128)S(1)}, f32[1,32,5]{2,1,0:T(8,128)S(1)}, u32[]{:S(2)}, u32[]{:S(2)}) %collective-permute-start.1) | collective-permute-done | bytes 672 | tf_op jit(solution)/shard_map/ppermute | solution.py:15
  50.3 0.8 %fusion.6 = f32[1,32,128]{2,1,0:T(8,128)} fusion(f32[1,32,128]{2,1,0:T(8,128)S(1)} %get-tuple-element.6, f32[1,32,5]{2,1,0:T(8,128)S(1)} %collective-permute-done.1, f32[1,32,5]{2,1,0:T(8,128)S(1)} %collective-permute-done, f32[1,11,32,128]{3,2,1,0:T(8,128)S(1)} %slice_divide_fusion), kind=kLoop, calls=%fused_computation.29 | loop fusion | flops 126976 | bytes 214272 | tf_op jit(solution)/shard_map/add | solution.py:40
  51.1 0.0 copy-done.1
  51.1 0.0 copy-done
Async XLA Ops:
  7.2 32.7 %reduce-scatter.2.cloned.1.call-start = ((), (), s32[]{:S(2)}) async-start(), calls=%async_computation.1 | async-start | bytes 1064960 | tf_op jit(solution)/shard_map/reduce_scatter | solution.py:32
  41.2 9.8 %copy-start.1 = (f32[1,32,128]{2,1,0:T(8,128)}, f32[1,32,128]{2,1,0:T(8,128)S(1)}, u32[]{:S(2)}) copy-start(f32[1,32,128]{2,1,0:T(8,128)S(1)} %get-tuple-element.6) | copy-start | bytes 49156
  41.3 6.3 %collective-permute-start = (f32[1,32,5]{2,1,0:T(8,128)S(1)}, f32[1,32,5]{2,1,0:T(8,128)S(1)}, u32[]{:S(2)}, u32[]{:S(2)}) collective-permute-start(f32[1,32,5]{2,1,0:T(8,128)S(1)} %get-tuple-element.8), channel_id=1, source_target_pairs={{0,2},{1,3},{4,6},{5,7},{8,10},{9,11},{12,14},{13,15},{16,18},{17,... | collective-permute-start | bytes 1928 | tf_op jit(solution)/shard_map/ppermute | solution.py:14
  44.7 5.6 %collective-permute-start.1 = (f32[1,32,5]{2,1,0:T(8,128)S(1)}, f32[1,32,5]{2,1,0:T(8,128)S(1)}, u32[]{:S(2)}, u32[]{:S(2)}) collective-permute-start(f32[1,32,5]{2,1,0:T(8,128)S(1)} %get-tuple-element.9), channel_id=1, source_target_pairs={{2,0},{3,1},{6,4},{7,5},{10,8},{11,9},{14,12},{15,13},{18,16},{19,... | collective-permute-start | bytes 1928 | tf_op jit(solution)/shard_map/ppermute | solution.py:15
  47.6 3.4 %copy-start = (f32[1,11,32,128]{3,2,1,0:T(8,128)}, f32[1,11,32,128]{3,2,1,0:T(8,128)S(1)}, u32[]{:S(2)}) copy-start(f32[1,11,32,128]{3,2,1,0:T(8,128)S(1)} %slice_divide_fusion) | copy-start | bytes 540676
Sparse Core Ops, SparseCore 0:
  12.9 26.9 reduce-scatter.1
where the time goes:
time: 58.4 us; the launch traced here: 57.9 us
  waiting for transfers between devices  29.7 us (51%)
  between operations  14.1 us (24%)
  other arithmetic  8.61 us (15%)
  starting transfers between devices  4.68 us (8%)
  local copies, waits for them, and re-layouts  0.8 us (1%)
    reduce_scatter x1, waiting for transfers between devices, local(): lax.psum_scatter(weighted_sums(masked, bands), 'fib', scatter_dimension=2...  27.1 us
    ppermute x1, starting transfers between devices, padded_2(): before = lax.ppermute(last, axis, up)  3.35 us
    ppermute x1, waiting for transfers between devices, padded_2(): after = lax.ppermute(leading, axis, down)  2.64 us
    reduce_sum x1, other arithmetic, weighted_sums(): band_sum = jnp.sum(weight[:, :, None] * bands.astype(jnp.float32), 0)  1.76 us
    div x1, other arithmetic, local(): flux_coadd = totals[:, 1] / ivar_coadd  1.34 us
    ppermute x1, starting transfers between devices, padded_2(): after = lax.ppermute(leading, axis, down)  1.29 us
  transfers between devices with their start and end apart: 3, of which 2 were waited for; matrix products, arithmetic and copies ran while one was open for 3% of the time, Pallas kernels for 0%

commit v1 on v0

v1 whole, which is shorter than its diff:
```python
import math

import jax
import jax.numpy as jnp
from jax import lax
from jax.experimental import pallas as pl
from jax.experimental.pallas import tpu as pltpu
from jax.sharding import PartitionSpec as P

HALO = 5
WEIGHT_MAX = 4.0
BAND_MAX = 0.2988282
HALF_MAX = 65000.0


def spectra_kernel(step_ref, spectra_ref, cover_ref, *outs):
    weight = spectra_ref[:, 0, 1].astype(jnp.float32) * cover_ref[...]
    flux = spectra_ref[:, 0, 0].astype(jnp.float32)
    pair = jnp.stack([jnp.sum(weight, 0), jnp.sum(weight * flux, 0)])
    step = pl.program_id(0)
    for slot, out in enumerate(outs):

        @pl.when(step == slot)
        def _():
            out[...] = pair


def bands_kernel(step_ref, spectra_ref, cover_ref, bands_ref, *outs):
    weight = spectra_ref[:, 0, 0].astype(jnp.float32) * cover_ref[...]
    step = pl.program_id(0)
    nbands = bands_ref.shape[2]
    for slot, out in enumerate(outs):

        @pl.when(step == slot)
        def _():
            for band in range(nbands):
                total = jnp.sum(weight * bands_ref[:, 0, band].astype(jnp.float32), 0)
                out[band] = total.astype(out.dtype)


def order_of(size):
    return sorted(range(1, size), key=lambda s: -min(s, size - s)) + [0]


def partial_sums(kernel, arrays, specs, shape, dtypes, targets, size):
    whole = pl.BlockSpec(shape, lambda g, t: (0,) * len(shape))
    return pl.pallas_call(
        kernel,
        out_shape=[jax.ShapeDtypeStruct(shape, d) for d in dtypes],
        grid_spec=pltpu.PrefetchScalarGridSpec(
            num_scalar_prefetch=1, grid=(size,), in_specs=specs, out_specs=[whole] * len(dtypes)
        ),
    )(targets, *arrays)


def local(spectra, bands, coverage):
    size = lax.axis_size("fib")
    exposures, _, nbands, fibers, width = bands.shape
    rows = fibers // size
    offsets = order_of(size)
    here = lax.axis_index("fib")
    targets = (here + jnp.array(offsets, jnp.int32)) % size
    cover = coverage.astype(jnp.float32)[:, :, None]
    cover_spec = pl.BlockSpec((exposures, rows, 1), lambda g, t: (0, t[g], 0))
    pairs = partial_sums(
        spectra_kernel,
        (spectra, cover),
        [pl.BlockSpec((exposures, 1, 2, rows, width), lambda g, t: (0, 0, 0, t[g], 0)), cover_spec],
        (2, rows, width),
        [jnp.float32] * size,
        targets,
        size,
    )
    sums = partial_sums(
        bands_kernel,
        (spectra, cover, bands),
        [
            pl.BlockSpec((exposures, 1, 1, rows, width), lambda g, t: (0, 0, 1, t[g], 0)),
            cover_spec,
            pl.BlockSpec((exposures, 1, nbands, rows, width), lambda g, t: (0, 0, 0, t[g], 0)),
        ],
        (nbands, rows, width),
        [jnp.float32] * size,
        targets,
        size,
    )

    def exchange(parts):
        return [
            lax.ppermute(part, "fib", [(i, (i + s) % size) for i in range(size)])
            for part, s in zip(parts, offsets[:-1])
        ]

    got_pairs = exchange(pairs[:-1])
    scale = 2.0 ** math.floor(math.log2(HALF_MAX / (exposures * WEIGHT_MAX * BAND_MAX)))
    got_sums = exchange([(s * scale).astype(jnp.float16) for s in sums[:-1]])
    pair = sum(got_pairs, pairs[-1])
    ivar = pair[0]
    flux = pair[1] / ivar
    before, after = halo(flux)
    padded = jnp.concatenate([before, flux, after], 1)
    total = sum([g.astype(jnp.float32) * (1 / scale) for g in got_sums], sums[-1])
    res = total / ivar
    model = sum(res[b] * padded[:, b : b + width] for b in range(nbands))
    return flux[None], ivar[None], res[None], model[None]


def halo(flux):
    size = lax.axis_size("wav")
    width = flux.shape[1]
    up = [(i, i + 1) for i in range(size - 1)]
    before = lax.ppermute(flux[:, width - HALO :], "wav", up)
    after = lax.ppermute(flux[:, :HALO], "wav", [(j, i) for i, j in up])
    return before, after


def solution(mesh):
    return jax.shard_map(
        local,
        mesh=mesh,
        in_specs=(
            P(("grp", "fib"), "arm", None, None, "wav"),
            P(("grp", "fib"), "arm", None, None, "wav"),
            P(("grp", "fib"), None),
        ),
        out_specs=(
            P("arm", ("grp", "fib"), "wav"),
            P("arm", ("grp", "fib"), "wav"),
            P("arm", None, ("grp", "fib"), "wav"),
            P("arm", ("grp", "fib"), "wav"),
        ),
        check_vma=False,
    )
```

time: 58.4 us -> 34.4 us (0.59)
  waiting for transfers between devices: 29.7 us -> 0.39 us
  between operations: 14.1 us -> 0.75 us
  starting transfers between devices: 4.68 us -> 17 us
  Pallas kernels: 0 us -> 7.68 us
  other arithmetic: 8.61 us -> 7.08 us
    reduce_scatter x1 -> x0, waiting for transfers between devices: 27.1 us -> none  [local(): lax.psum_scatter(weighted_sums(masked, bands), 'fib', scatter_dimension=2...]
    ppermute x2 -> x8, starting transfers between devices: 4.64 us -> 17 us  [the longest x6 11.1 us: exchange(): lax.ppermute(part, 'fib', [(i, (i + s) % size) for i in range(size)])]
    pallas_call x0 -> x2, Pallas kernels: none -> 7.68 us  [partial_sums(): pl.pallas_call(kernel, out_shape=[jax.ShapeDtypeStruct(shape, d) for d in...]
    reduce_sum x2 -> x0, other arithmetic: 2.88 us -> none  [the longest x1 1.76 us: weighted_sums(): band_sum = jnp.sum(weight[:, :, None] * bands.astype(jnp.float32), 0)]
    ppermute x2 -> x8, waiting for transfers between devices: 2.65 us -> 0.39 us  [the longest x1 0.37 us: halo(): before = lax.ppermute(flux[:, width - HALO:], 'wav', up)]
    convert_element_type x1 -> x3, other arithmetic: 0.69 us -> 2.83 us  [local(): got_sums = exchange([(s * scale).astype(jnp.float16) for s in sums[:-1]])]
    broadcast_in_dim x0 -> x2, other arithmetic: none -> 1.44 us  [the longest x1 0.76 us: local(): return (flux[None], ivar[None], res[None], model[None])]
    select_n x0 -> x1, other arithmetic: none -> 1.17 us  [local(): targets = (here + jnp.array(offsets, jnp.int32)) % size]
  transfers between devices with their start and end apart: 3 -> 8, of which waited for: 2 -> 1; matrix products, arithmetic and copies ran while one was open for 3% -> 13% of each run, Pallas kernels for 0% -> 13%
where the time goes in v1:
time: 34.4 us; the launch traced here: 33.8 us
  starting transfers between devices  17 us (49%)
  Pallas kernels  7.68 us (22%)
  other arithmetic  7.08 us (21%)
  local copies, waits for them, and re-layouts  0.95 us (3%)
  between operations  0.75 us (2%)
  waiting for transfers between devices  0.39 us (1%)
    ppermute x6, starting transfers between devices, exchange(): lax.ppermute(part, 'fib', [(i, (i + s) % size) for i in range(size)])  11.1 us
    pallas_call x2, Pallas kernels, partial_sums(): pl.pallas_call(kernel, out_shape=[jax.ShapeDtypeStruct(shape, d) for d in...  7.68 us
    ppermute x1, starting transfers between devices, halo(): before = lax.ppermute(flux[:, width - HALO:], 'wav', up)  4.54 us
    convert_element_type x3, other arithmetic, local(): got_sums = exchange([(s * scale).astype(jnp.float16) for s in sums[:-1]])  2.83 us
    ppermute x1, starting transfers between devices, halo(): after = lax.ppermute(flux[:, :HALO], 'wav', [(j, i) for i, j in up])  1.28 us
    select_n x1, other arithmetic, local(): targets = (here + jnp.array(offsets, jnp.int32)) % size  1.17 us
    div x1, other arithmetic, local(): res = total / ivar  1 us
    broadcast_in_dim x1, local copies, waits for them, and re-layouts, local(): cover = coverage.astype(jnp.float32)[:, :, None]  0.86 us
  transfers between devices with their start and end apart: 8, of which 1 were waited for; matrix products, arithmetic and copies ran while one was open for 13% of the time, Pallas kernels for 13%

profile of v1, /device:TPU:0, one launch (start us, length us, event | category | flops | bytes accessed | tf_op | source)
XLA Modules:
  0.0 33.8 jit_solution(5620282370318478894)
XLA Ops:
  0.6 0.7 %convert_bitcast_fusion = f32[4,128,1]{1,0,2:T(4,128)S(1)} fusion(s32[4,128]{1,0:T(4,128)} %param.6), kind=kLoop, calls=%fused_computation.68 | loop fusion | flops 512 | bytes 4096 | tf_op jit(solution)/shard_map/broadcast_in_dim | solution.py:63
  1.3 0.9 %copy.8.cover_ref = f32[4,128,1]{2,1,0:T(8,128)} copy(f32[4,128,1]{1,0,2:T(4,128)S(1)} %convert_bitcast_fusion) | data formatting | bytes 4096 | tf_op jit(solution)/shard_map/broadcast_in_dim | solution.py:63
  2.2 1.2 %and_select_fusion.step_ref = s32[4]{0:T(128)} fusion(s32[4]{0:T(128)} %constant.26.clone, s32[]{:T(128)S(6)} %axis_index.15), kind=kLoop, calls=%fused_computation.69 | loop fusion | flops 48 | bytes 36 | tf_op jit(solution)/shard_map/jit(remainder)/select_n | solution.py:62
  3.4 3.4 %shard_map.75 = (f32[2,32,128]{2,1,0:T(8,128)}, f32[2,32,128]{2,1,0:T(8,128)}, f32[2,32,128]{2,1,0:T(8,128)}, f32[2,32,128]{2,1,0:T(8,128)}) custom-call(s32[4]{0:T(128)} %and_select_fusion.step_ref, bf16[4,1,2,128,128]{4,3,2,1,0:T(8,128)(2,1)} %spectra_ref.3, f32[4,128,1]{2,1,0:T(8,128)} %copy.8.cover_ref), custom_call_target="tpu_custom_call" | custom-call | tf_op jit(solution)/shard_map/pallas_call | solution.py:47
  6.8 5.1 %collective-permute-start.2 = (f32[2,32,128]{2,1,0:T(8,128)}, f32[2,32,128]{2,1,0:T(8,128)S(1)}, u32[]{:S(2)}, u32[]{:S(2)}) collective-permute-start(f32[2,32,128]{2,1,0:T(8,128)} %get-tuple-element.15), channel_id=1, source_target_pairs={{0,12},{4,0},{8,4},{12,8},{1,13},{5,1},{9,5},{13,9},{2,14},{6,2},{... | collective-permute-start | bytes 98312 | tf_op jit(solution)/shard_map/ppermute | solution.py:90
  11.9 0.0 collective-permute-start.1
  11.9 1.0 %collective-permute-start = (f32[2,32,128]{2,1,0:T(8,128)}, f32[2,32,128]{2,1,0:T(8,128)S(1)}, u32[]{:S(2)}, u32[]{:S(2)}) collective-permute-start(f32[2,32,128]{2,1,0:T(8,128)} %get-tuple-element.13), channel_id=1, source_target_pairs={{0,8},{4,12},{8,0},{12,4},{1,9},{5,13},{9,1},{13,5},{2,10},{6,14},... | collective-permute-start | bytes 98312 | tf_op jit(solution)/shard_map/ppermute | solution.py:90
  12.9 4.2 %shard_map.76 = (f32[11,32,128]{2,1,0:T(8,128)}, f32[11,32,128]{2,1,0:T(8,128)}, f32[11,32,128]{2,1,0:T(8,128)}, f32[11,32,128]{2,1,0:T(8,128)}) custom-call(s32[4]{0:T(128)} %and_select_fusion.step_ref, bf16[4,1,2,128,128]{4,3,2,1,0:T(8,128)(2,1)} %spectra_ref.3, f32[4,128,1]{2,1,0:T(8,128)} %copy.8.cover_ref, bf16[4,1,11,128,128]{4,3,2,1,0:T(8,128)(2,1)} %bands_ref.1), custom_call_target="tpu_custom_call" | custom-call | tf_op jit(solution)/shard_map/pallas_call | solution.py:47
  17.2 0.9 %multiply_convert_fusion = f16[11,32,128]{2,1,0:T(8,128)(2,1)S(1)} fusion(f32[11,32,128]{2,1,0:T(8,128)} %get-tuple-element.19), kind=kLoop, calls=%fused_computation.1 | loop fusion | flops 90112 | bytes 270336 | tf_op jit(solution)/shard_map/convert_element_type | solution.py:96
  18.1 2.9 %collective-permute-start.5 = (f16[11,32,128]{2,1,0:T(8,128)(2,1)S(1)}, f16[11,32,128]{2,1,0:T(8,128)(2,1)S(1)}, u32[]{:S(2)}, u32[]{:S(2)}) collective-permute-start(f16[11,32,128]{2,1,0:T(8,128)(2,1)S(1)} %multiply_convert_fusion), channel_id=1, source_target_pairs={{0,12},{4,0},{8,4},{12,8},{1,13},{5,1},{9,5},{13,9},{2,14},{6,2},{... | collective-permute-start | bytes 270344 | tf_op jit(solution)/shard_map/ppermute | solution.py:90
  21.0 0.9 %multiply_convert_fusion.1 = f16[11,32,128]{2,1,0:T(8,128)(2,1)S(1)} fusion(f32[11,32,128]{2,1,0:T(8,128)} %get-tuple-element.18), kind=kLoop, calls=%fused_computation.2 | loop fusion | flops 90112 | bytes 270336 | tf_op jit(solution)/shard_map/convert_element_type | solution.py:96
  21.9 0.6 %collective-permute-start.4 = (f16[11,32,128]{2,1,0:T(8,128)(2,1)S(1)}, f16[11,32,128]{2,1,0:T(8,128)(2,1)S(1)}, u32[]{:S(2)}, u32[]{:S(2)}) collective-permute-start(f16[11,32,128]{2,1,0:T(8,128)(2,1)S(1)} %multiply_convert_fusion.1), channel_id=1, source_target_pairs={{0,4},{4,8},{8,12},{12,0},{1,5},{5,9},{9,13},{13,1},{2,6},{6,10},{... | collective-permute-start | bytes 270344 | tf_op jit(solution)/shard_map/ppermute | solution.py:90
  22.6 0.9 %multiply_convert_fusion.2 = f16[11,32,128]{2,1,0:T(8,128)(2,1)S(1)} fusion(f32[11,32,128]{2,1,0:T(8,128)} %get-tuple-element.17), kind=kLoop, calls=%fused_computation.3 | loop fusion | flops 90112 | bytes 270336 | tf_op jit(solution)/shard_map/convert_element_type | solution.py:96
  23.5 0.0 collective-permute-done.2
  23.5 1.5 %collective-permute-start.3 = (f16[11,32,128]{2,1,0:T(8,128)(2,1)S(1)}, f16[11,32,128]{2,1,0:T(8,128)(2,1)S(1)}, u32[]{:S(2)}, u32[]{:S(2)}) collective-permute-start(f16[11,32,128]{2,1,0:T(8,128)(2,1)S(1)} %multiply_convert_fusion.2), channel_id=1, source_target_pairs={{0,8},{4,12},{8,0},{12,4},{1,9},{5,13},{9,1},{13,5},{2,10},{6,14},... | collective-permute-start | bytes 270344 | tf_op jit(solution)/shard_map/ppermute | solution.py:90
  25.1 0.0 copy-start.1
  25.1 0.6 %slice_divide_fusion = f32[1,32,128]{2,1,0:T(8,128)} fusion(f32[1,32,128]{2,1,0:T(8,128)S(1)} %get-tuple-element.21, f32[2,32,128]{2,1,0:T(8,128)S(1)} %add_add_fusion), kind=kLoop, calls=%fused_computation.65 | loop fusion | flops 4096 | bytes 49152 | tf_op jit(solution)/shard_map/div | solution.py:99
  25.7 0.1 fusion.31
  25.8 1.3 %collective-permute-start.7 = (f32[32,5]{1,0:T(8,128)S(1)}, f32[32,5]{1,0:T(8,128)S(1)}, u32[]{:S(2)}, u32[]{:S(2)}) collective-permute-start(f32[32,5]{1,0:T(8,128)S(1)} %get-tuple-element.23), channel_id=1, source_target_pairs={{2,0},{3,1},{6,4},{7,5},{10,8},{11,9},{14,12},{15,13},{18,16},{19,... | collective-permute-start | bytes 1928 | tf_op jit(solution)/shard_map/ppermute | solution.py:113
  27.1 4.5 %collective-permute-start.6 = (f32[32,5]{1,0:T(8,128)S(1)}, f32[32,5]{1,0:T(8,128)S(1)}, u32[]{:S(2)}, u32[]{:S(2)}) collective-permute-start(f32[32,5]{1,0:T(8,128)S(1)} %get-tuple-element.22), channel_id=1, source_target_pairs={{0,2},{1,3},{4,6},{5,7},{8,10},{9,11},{12,14},{13,15},{16,18},{17,... | collective-permute-start | bytes 1928 | tf_op jit(solution)/shard_map/ppermute | solution.py:112
  31.7 1.0 %add_divide_fusion = f32[11,32,128]{2,1,0:T(8,128)S(1)} fusion(f16[11,32,128]{2,1,0:T(8,128)(2,1)S(1)} %collective-permute-done.5, f16[11,32,128]{2,1,0:T(8,128)(2,1)S(1)} %collective-permute-done.4, f32[11,32,128]{2,1,0:T(8,128)} %get-tuple-element.16, f16[11,32,128]{2,1,0:T(8,128)(2,1)S(1)} %collective-permute-done.3, f32[32,128]{1,0:T(8,128)S(1)} %bitcast.56), kind=kLoop, calls=%fused_computation | loop fusion | flops 450560 | bytes 647168 | tf_op jit(solution)/shard_map/div | solution.py:103
  32.7 0.0 copy-start
  32.7 0.4 %collective-permute-done.6 = f32[32,5]{1,0:T(8,128)S(1)} collective-permute-done((f32[32,5]{1,0:T(8,128)S(1)}, f32[32,5]{1,0:T(8,128)S(1)}, u32[]{:S(2)}, u32[]{:S(2)}) %collective-permute-start.6) | collective-permute-done | bytes 672 | tf_op jit(solution)/shard_map/ppermute | solution.py:112
  33.1 0.8 %fusion.4 = f32[1,32,128]{2,1,0:T(8,128)} fusion(f32[32,128]{1,0:T(8,128)S(1)} %get-tuple-element.20, f32[32,5]{1,0:T(8,128)S(1)} %collective-permute-done.7, f32[32,5]{1,0:T(8,128)S(1)} %collective-permute-done.6, f32[11,32,128]{2,1,0:T(8,128)S(1)} %add_divide_fusion), kind=kLoop, calls=%fused_computation.25 | loop fusion | flops 126976 | bytes 214272 | tf_op jit(solution)/shard_map/broadcast_in_dim | solution.py:105
  (12 shorter events, 0.0 us)
Async XLA Ops:
  6.8 18.2 %copy-start.2 = (f32[2,32,128]{2,1,0:T(8,128)S(1)}, f32[2,32,128]{2,1,0:T(8,128)}, u32[]{:S(2)}) copy-start(f32[2,32,128]{2,1,0:T(8,128)} %get-tuple-element.12) | copy-start | bytes 98308
  6.8 16.7 %collective-permute-start.2 = (f32[2,32,128]{2,1,0:T(8,128)}, f32[2,32,128]{2,1,0:T(8,128)S(1)}, u32[]{:S(2)}, u32[]{:S(2)}) collective-permute-start(f32[2,32,128]{2,1,0:T(8,128)} %get-tuple-element.15), channel_id=1, source_target_pairs={{0,12},{4,0},{8,4},{12,8},{1,13},{5,1},{9,5},{13,9},{2,14},{6,2},{... | collective-permute-start | bytes 98312 | tf_op jit(solution)/shard_map/ppermute | solution.py:90
  11.9 13.1 %collective-permute-start.1 = (f32[2,32,128]{2,1,0:T(8,128)}, f32[2,32,128]{2,1,0:T(8,128)S(1)}, u32[]{:S(2)}, u32[]{:S(2)}) collective-permute-start(f32[2,32,128]{2,1,0:T(8,128)} %get-tuple-element.14), channel_id=1, source_target_pairs={{0,4},{4,8},{8,12},{12,0},{1,5},{5,9},{9,13},{13,1},{2,6},{6,10},{... | collective-permute-start | bytes 98312 | tf_op jit(solution)/shard_map/ppermute | solution.py:90
  11.9 13.1 %collective-permute-start = (f32[2,32,128]{2,1,0:T(8,128)}, f32[2,32,128]{2,1,0:T(8,128)S(1)}, u32[]{:S(2)}, u32[]{:S(2)}) collective-permute-start(f32[2,32,128]{2,1,0:T(8,128)} %get-tuple-element.13), channel_id=1, source_target_pairs={{0,8},{4,12},{8,0},{12,4},{1,9},{5,13},{9,1},{13,5},{2,10},{6,14},... | collective-permute-start | bytes 98312 | tf_op jit(solution)/shard_map/ppermute | solution.py:90
  18.1 13.5 %collective-permute-start.5 = (f16[11,32,128]{2,1,0:T(8,128)(2,1)S(1)}, f16[11,32,128]{2,1,0:T(8,128)(2,1)S(1)}, u32[]{:S(2)}, u32[]{:S(2)}) collective-permute-start(f16[11,32,128]{2,1,0:T(8,128)(2,1)S(1)} %multiply_convert_fusion), channel_id=1, source_target_pairs={{0,12},{4,0},{8,4},{12,8},{1,13},{5,1},{9,5},{13,9},{2,14},{6,2},{... | collective-permute-start | bytes 270344 | tf_op jit(solution)/shard_map/ppermute | solution.py:90
  21.9 9.7 %collective-permute-start.4 = (f16[11,32,128]{2,1,0:T(8,128)(2,1)S(1)}, f16[11,32,128]{2,1,0:T(8,128)(2,1)S(1)}, u32[]{:S(2)}, u32[]{:S(2)}) collective-permute-start(f16[11,32,128]{2,1,0:T(8,128)(2,1)S(1)} %multiply_convert_fusion.1), channel_id=1, source_target_pairs={{0,4},{4,8},{8,12},{12,0},{1,5},{5,9},{9,13},{13,1},{2,6},{6,10},{... | collective-permute-start | bytes 270344 | tf_op jit(solution)/shard_map/ppermute | solution.py:90
  23.5 8.1 %collective-permute-start.3 = (f16[11,32,128]{2,1,0:T(8,128)(2,1)S(1)}, f16[11,32,128]{2,1,0:T(8,128)(2,1)S(1)}, u32[]{:S(2)}, u32[]{:S(2)}) collective-permute-start(f16[11,32,128]{2,1,0:T(8,128)(2,1)S(1)} %multiply_convert_fusion.2), channel_id=1, source_target_pairs={{0,8},{4,12},{8,0},{12,4},{1,9},{5,13},{9,1},{13,5},{2,10},{6,14},... | collective-permute-start | bytes 270344 | tf_op jit(solution)/shard_map/ppermute | solution.py:90
  25.1 8.7 %copy-start.1 = (f32[1,32,128]{2,1,0:T(8,128)}, f32[1,32,128]{2,1,0:T(8,128)S(1)}, u32[]{:S(2)}) copy-start(f32[1,32,128]{2,1,0:T(8,128)S(1)} %get-tuple-element.21) | copy-start | bytes 49156
  25.8 6.9 %collective-permute-start.7 = (f32[32,5]{1,0:T(8,128)S(1)}, f32[32,5]{1,0:T(8,128)S(1)}, u32[]{:S(2)}, u32[]{:S(2)}) collective-permute-start(f32[32,5]{1,0:T(8,128)S(1)} %get-tuple-element.23), channel_id=1, source_target_pairs={{2,0},{3,1},{6,4},{7,5},{10,8},{11,9},{14,12},{15,13},{18,16},{19,... | collective-permute-start | bytes 1928 | tf_op jit(solution)/shard_map/ppermute | solution.py:113
  27.1 6.0 %collective-permute-start.6 = (f32[32,5]{1,0:T(8,128)S(1)}, f32[32,5]{1,0:T(8,128)S(1)}, u32[]{:S(2)}, u32[]{:S(2)}) collective-permute-start(f32[32,5]{1,0:T(8,128)S(1)} %get-tuple-element.22), channel_id=1, source_target_pairs={{0,2},{1,3},{4,6},{5,7},{8,10},{9,11},{12,14},{13,15},{16,18},{17,... | collective-permute-start | bytes 1928 | tf_op jit(solution)/shard_map/ppermute | solution.py:112
  32.7 1.2 %copy-start = (f32[11,32,128]{2,1,0:T(8,128)}, f32[11,32,128]{2,1,0:T(8,128)S(1)}, u32[]{:S(2)}) copy-start(f32[11,32,128]{2,1,0:T(8,128)S(1)} %add_divide_fusion) | copy-start | bytes 540676

commit v2 on v1

v2 whole, which is shorter than its diff:
```python
import math

import jax
import jax.numpy as jnp
from jax import lax
from jax.experimental import pallas as pl
from jax.experimental.pallas import tpu as pltpu
from jax.sharding import PartitionSpec as P

HALO = 5
WEIGHT_MAX = 4.0
BAND_MAX = 0.2988282
HALF_MAX = 65000.0


def order_of(size):
    return sorted(range(1, size), key=lambda s: -min(s, size - s)) + [0]


def sums_kernel(cover_ref, spectra_hbm, bands_hbm, *refs, offsets, scale):
    size = len(offsets)
    pairs, sums = refs[:size], refs[size : 2 * size]
    spectra, bands, weight, spectra_sem, bands_sem = refs[2 * size :]
    exposures, nbands, fibers, width = bands.shape
    rows = fibers // size
    here = lax.axis_index("fib")
    starts = [pl.multiple_of((here + s) % size * rows, rows) for s in offsets]
    copies = [pltpu.make_async_copy(spectra_hbm.at[:, 0], spectra, spectra_sem)]
    for slot, start in enumerate(starts):
        part = pl.ds(start, rows)
        copies.append(
            pltpu.make_async_copy(bands_hbm.at[:, 0, :, part], bands.at[:, :, part], bands_sem.at[slot])
        )
    for copy in copies:
        copy.start()
    cover = cover_ref[...].astype(jnp.float32)
    copies[0].wait()
    for e in range(exposures):
        column = jnp.broadcast_to(cover[e : e + 1], (width, fibers)).T
        weight[e] = spectra[e, 1].astype(jnp.float32) * column
    for slot, start in enumerate(starts):
        part = pl.ds(start, rows)
        part_weight = [weight[e, part] for e in range(exposures)]
        pairs[slot][0] = sum(part_weight[1:], part_weight[0])
        pairs[slot][1] = sum(part_weight[e] * spectra[e, 0, part].astype(jnp.float32) for e in range(exposures))
    for slot, start in enumerate(starts):
        part = pl.ds(start, rows)
        part_weight = [weight[e, part] for e in range(exposures)]
        copies[slot + 1].wait()
        for band in range(nbands):
            total = sum(part_weight[e] * bands[e, band, part].astype(jnp.float32) for e in range(exposures))
            sums[slot][band] = total * scale if slot < size - 1 else total


def partial_sums(spectra, bands, coverage, offsets, scale):
    size = len(offsets)
    exposures, _, nbands, fibers, width = bands.shape
    rows = fibers // size
    vmem = pl.BlockSpec(memory_space=pltpu.VMEM)
    hbm = pl.BlockSpec(memory_space=pl.ANY)
    shapes = [(2, rows, width)] * size + [(nbands, rows, width)] * size
    outs = pl.pallas_call(
        lambda *refs: sums_kernel(*refs, offsets=offsets, scale=scale),
        out_shape=[pltpu.VMEM(s, jnp.float32) for s in shapes],
        in_specs=[vmem, hbm, hbm],
        out_specs=[vmem] * (2 * size),
        scratch_shapes=[
            pltpu.VMEM((exposures, 2, fibers, width), jnp.bfloat16),
            pltpu.VMEM((exposures, nbands, fibers, width), jnp.bfloat16),
            pltpu.VMEM((exposures, fibers, width), jnp.float32),
            pltpu.SemaphoreType.DMA,
            pltpu.SemaphoreType.DMA((size,)),
        ],
        name="partial_sums",
    )(coverage, spectra, bands)
    return outs[:size], outs[size:]


def local(spectra, bands, coverage):
    size = lax.axis_size("fib")
    exposures, _, nbands, fibers, width = bands.shape
    offsets = order_of(size)
    scale = 2.0 ** math.floor(math.log2(HALF_MAX / (exposures * WEIGHT_MAX * BAND_MAX)))
    pairs, sums = partial_sums(spectra, bands, coverage, offsets, scale)

    def exchange(parts):
        return [
            lax.ppermute(part, "fib", [(i, (i + s) % size) for i in range(size)])
            for part, s in zip(parts, offsets[:-1])
        ]

    got_pairs = exchange(pairs[:-1])
    got_sums = exchange([s.astype(jnp.float16) for s in sums[:-1]])
    pair = sum(got_pairs, pairs[-1])
    ivar = pair[0]
    flux = pair[1] / ivar
    before, after = halo(flux)
    padded = jnp.concatenate([before, flux, after], 1)
    total = sum([g.astype(jnp.float32) * (1 / scale) for g in got_sums], sums[-1])
    res = total / ivar
    model = sum(res[b] * padded[:, b : b + width] for b in range(nbands))
    return flux[None], ivar[None], res[None], model[None]


def halo(flux):
    size = lax.axis_size("wav")
    width = flux.shape[1]
    first, last = flux[:, :HALO], flux[:, width - HALO :]
    if size == 2:
        low = lax.axis_index("wav") == 0
        got = lax.ppermute(jnp.where(low, last, first), "wav", [(0, 1), (1, 0)])
        return jnp.where(low, 0.0, got), jnp.where(low, got, 0.0)
    up = [(i, i + 1) for i in range(size - 1)]
    return lax.ppermute(last, "wav", up), lax.ppermute(first, "wav", [(j, i) for i, j in up])


def solution(mesh):
    return jax.shard_map(
        local,
        mesh=mesh,
        in_specs=(
            P(("grp", "fib"), "arm", None, None, "wav"),
            P(("grp", "fib"), "arm", None, None, "wav"),
            P(("grp", "fib"), None),
        ),
        out_specs=(
            P("arm", ("grp", "fib"), "wav"),
            P("arm", ("grp", "fib"), "wav"),
            P("arm", None, ("grp", "fib"), "wav"),
            P("arm", ("grp", "fib"), "wav"),
        ),
        check_vma=False,
    )
```

time: 34.4 us -> 20.5 us (0.60); the launches traced: 33.8 us -> 20.4 us
  Pallas kernels: 7.68 us -> 2.19 us
  other arithmetic: 7.08 us -> 1.59 us
  starting transfers between devices: 17 us -> 13.5 us
  waiting for transfers between devices: 0.39 us -> 2.4 us
  local copies, waits for them, and re-layouts: 0.95 us -> 0.01 us
    pallas_call x2 -> x1, Pallas kernels: 7.68 us -> 2.19 us  [partial_sums(): pl.pallas_call(lambda *refs: sums_kernel(*refs, offsets=offsets, scale=sc...]
    ppermute x2 -> x1, starting transfers between devices: 5.82 us -> 1.5 us  [halo(): got = lax.ppermute(jnp.where(low, last, first), 'wav', [(0, 1), (1, 0)])]
    convert_element_type x3, other arithmetic: 2.83 us -> 0.05 us  [local(): got_sums = exchange([s.astype(jnp.float16) for s in sums[:-1]])]
    ppermute x2 -> x1, waiting for transfers between devices: 0.37 us -> 1.63 us  [halo(): got = lax.ppermute(jnp.where(low, last, first), 'wav', [(0, 1), (1, 0)])]
    select_n x1 -> x2, other arithmetic: 1.17 us -> 0.08 us  [the longest x1 0.07 us: halo(): got = lax.ppermute(jnp.where(low, last, first), 'wav', [(0, 1), (1, 0)])]
    div x1, other arithmetic: 1 us -> 0.07 us  [local(): res = total / ivar]
    broadcast_in_dim x1 -> x0, local copies, waits for them, and re-layouts: 0.86 us -> none  [local(): cover = coverage.astype(jnp.float32)[:, :, None]]
    ppermute x6, starting transfers between devices: 11.1 us -> 12 us  [exchange(): lax.ppermute(part, 'fib', [(i, (i + s) % size) for i in range(size)])]
  transfers between devices with their start and end apart: 8 -> 7, of which waited for: 1 -> 3; matrix products, arithmetic and copies ran while one was open for 13% -> 4% of each run, Pallas kernels for 13% -> 0%
where the time goes in v2:
time: 20.5 us; the launch traced here: 20.4 us
  starting transfers between devices  13.5 us (66%)
  waiting for transfers between devices  2.4 us (12%)
  Pallas kernels  2.19 us (11%)
  other arithmetic  1.59 us (8%)
  between operations  0.72 us (4%)
    ppermute x6, starting transfers between devices, exchange(): lax.ppermute(part, 'fib', [(i, (i + s) % size) for i in range(size)])  12 us
    pallas_call x1, Pallas kernels, partial_sums(): pl.pallas_call(lambda *refs: sums_kernel(*refs, offsets=offsets, scale=sc...  2.19 us
    ppermute x1, waiting for transfers between devices, halo(): got = lax.ppermute(jnp.where(low, last, first), 'wav', [(0, 1), (1, 0)])  1.63 us
    ppermute x1, starting transfers between devices, halo(): got = lax.ppermute(jnp.where(low, last, first), 'wav', [(0, 1), (1, 0)])  1.5 us
    ppermute x6, waiting for transfers between devices, exchange(): lax.ppermute(part, 'fib', [(i, (i + s) % size) for i in range(size)])  0.77 us
    broadcast_in_dim x1, other arithmetic, local(): return (flux[None], ivar[None], res[None], model[None])  0.76 us
    div x2, other arithmetic, local(): flux = pair[1] / ivar  0.62 us
  transfers between devices with their start and end apart: 7, of which 3 were waited for; matrix products, arithmetic and copies ran while one was open for 4% of the time, Pallas kernels for 0%

profile of v2, /device:TPU:0, one launch (start us, length us, event | category | flops | bytes accessed | tf_op | source)
XLA Modules:
  0.0 20.4 jit_solution(17236137940243895876)
XLA Ops:
  0.6 2.2 %partial_sums.1 = (f32[2,32,128]{2,1,0:T(8,128)S(1)}, f32[2,32,128]{2,1,0:T(8,128)S(1)}, f32[2,32,128]{2,1,0:T(8,128)S(1)}, f32[2,32,128]{2,1,0:T(8,128)S(1)}, f...) custom-call(s32[4,128]{1,0:T(4,128)} %refs_0_.1, ...), custom_call_target="tpu_custom_call" | custom-call | tf_op jit(solution)/shard_map/partial_sums/pallas_call | solution.py:62
  2.8 4.1 %collective-permute-start = (f32[2,32,128]{2,1,0:T(8,128)S(1)}, f32[2,32,128]{2,1,0:T(8,128)S(1)}, u32[]{:S(2)}, u32[]{:S(2)}) collective-permute-start(f32[2,32,128]{2,1,0:T(8,128)S(1)} %get-tuple-element.13), channel_id=1, source_target_pairs={{0,8},{4,12},{8,0},{12,4},{1,9},{5,13},{9,1},{13,5},{2,10},{6,14},... | collective-permute-start | bytes 98312 | tf_op jit(solution)/shard_map/ppermute | solution.py:88
  7.0 1.6 %collective-permute-start.1 = (f32[2,32,128]{2,1,0:T(8,128)S(1)}, f32[2,32,128]{2,1,0:T(8,128)S(1)}, u32[]{:S(2)}, u32[]{:S(2)}) collective-permute-start(f32[2,32,128]{2,1,0:T(8,128)S(1)} %get-tuple-element.14), channel_id=1, source_target_pairs={{0,4},{4,8},{8,12},{12,0},{1,5},{5,9},{9,13},{13,1},{2,6},{6,10},{... | collective-permute-start | bytes 98312 | tf_op jit(solution)/shard_map/ppermute | solution.py:88
  8.5 2.2 %collective-permute-start.2 = (f32[2,32,128]{2,1,0:T(8,128)S(1)}, f32[2,32,128]{2,1,0:T(8,128)S(1)}, u32[]{:S(2)}, u32[]{:S(2)}) collective-permute-start(f32[2,32,128]{2,1,0:T(8,128)S(1)} %get-tuple-element.15), channel_id=1, source_target_pairs={{0,12},{4,0},{8,4},{12,8},{1,13},{5,1},{9,5},{13,9},{2,14},{6,2},{... | collective-permute-start | bytes 98312 | tf_op jit(solution)/shard_map/ppermute | solution.py:88
  10.8 0.1 collective-permute-start.3
  10.9 0.6 %collective-permute-start.4 = (f16[11,32,128]{2,1,0:T(8,128)(2,1)S(1)}, f16[11,32,128]{2,1,0:T(8,128)(2,1)S(1)}, u32[]{:S(2)}, u32[]{:S(2)}) collective-permute-start(f16[11,32,128]{2,1,0:T(8,128)(2,1)S(1)} %convert_element_type.20), channel_id=1, source_target_pairs={{0,4},{4,8},{8,12},{12,0},{1,5},{5,9},{9,13},{13,1},{2,6},{6,10},{... | collective-permute-start | bytes 270344 | tf_op jit(solution)/shard_map/ppermute | solution.py:88
  11.5 0.0 collective-permute-done
  11.5 3.3 %collective-permute-start.5 = (f16[11,32,128]{2,1,0:T(8,128)(2,1)S(1)}, f16[11,32,128]{2,1,0:T(8,128)(2,1)S(1)}, u32[]{:S(2)}, u32[]{:S(2)}) collective-permute-start(f16[11,32,128]{2,1,0:T(8,128)(2,1)S(1)} %convert_element_type.22), channel_id=1, source_target_pairs={{0,12},{4,0},{8,4},{12,8},{1,13},{5,1},{9,5},{13,9},{2,14},{6,2},{... | collective-permute-start | bytes 270344 | tf_op jit(solution)/shard_map/ppermute | solution.py:88
  14.9 0.0 collective-permute-done.1
  14.9 0.0 collective-permute-done.2
  14.9 0.0 copy-start.1
  14.9 0.1 slice_select_fusion
  15.0 1.5 %collective-permute-start.6 = (f32[32,5]{1,0:T(8,128)S(1)}, f32[32,5]{1,0:T(8,128)S(1)}, u32[]{:S(2)}, u32[]{:S(2)}) collective-permute-start(f32[32,5]{1,0:T(8,128)S(1)} %slice_select_fusion), channel_id=1, source_target_pairs={{0,2},{2,0},{1,3},{3,1},{4,6},{6,4},{5,7},{7,5},{8,10},{10,8},{9,1... | collective-permute-start | bytes 1928 | tf_op jit(solution)/shard_map/ppermute | solution.py:111
  16.5 0.6 %slice_divide_fusion = f32[1,32,128]{2,1,0:T(8,128)} fusion(f32[1,32,128]{2,1,0:T(8,128)S(1)} %get-tuple-element.21, f32[2,32,128]{2,1,0:T(8,128)S(1)} %add_add_fusion), kind=kLoop, calls=%fused_computation.63 | loop fusion | flops 4096 | bytes 49152 | tf_op jit(solution)/shard_map/div | solution.py:96
  17.1 1.6 %collective-permute-done.6 = f32[32,5]{1,0:T(8,128)S(1)} collective-permute-done((f32[32,5]{1,0:T(8,128)S(1)}, f32[32,5]{1,0:T(8,128)S(1)}, u32[]{:S(2)}, u32[]{:S(2)}) %collective-permute-start.6) | collective-permute-done | bytes 672 | tf_op jit(solution)/shard_map/ppermute | solution.py:111
  18.8 0.4 %collective-permute-done.3 = f16[11,32,128]{2,1,0:T(8,128)(2,1)S(1)} collective-permute-done((f16[11,32,128]{2,1,0:T(8,128)(2,1)S(1)}, f16[11,32,128]{2,1,0:T(8,128)(2,1)S(1)}, u32[]{:S(2)}, u32[]{:S(2)}) %collective-permute-start.3) | collective-permute-done | bytes 90144 | tf_op jit(solution)/shard_map/ppermute | solution.py:88
  19.2 0.0 collective-permute-done.4
  19.2 0.3 %collective-permute-done.5 = f16[11,32,128]{2,1,0:T(8,128)(2,1)S(1)} collective-permute-done((f16[11,32,128]{2,1,0:T(8,128)(2,1)S(1)}, f16[11,32,128]{2,1,0:T(8,128)(2,1)S(1)}, u32[]{:S(2)}, u32[]{:S(2)}) %collective-permute-start.5) | collective-permute-done | bytes 90144 | tf_op jit(solution)/shard_map/ppermute | solution.py:88
  19.5 0.1 add_divide_fusion
  19.6 0.0 copy-start
  19.6 0.8 %fusion.4 = f32[1,32,128]{2,1,0:T(8,128)} fusion(f32[32,128]{1,0:T(8,128)S(1)} %get-tuple-element.20, f32[32,5]{1,0:T(8,128)S(1)} %get-tuple-element.23, f32[32,5]{1,0:T(8,128)S(1)} %get-tuple-element.22, f32[11,32,128]{2,1,0:T(8,128)S(1)} %add_divide_fusion), kind=kLoop, calls=%fused_computation.22 | loop fusion | flops 126976 | bytes 214272 | tf_op jit(solution)/shard_map/broadcast_in_dim | solution.py:102
  20.4 0.0 copy-done.1
  20.4 0.0 copy-done
  (6 shorter events, 0.1 us)
Async XLA Ops:
  2.8 8.7 %collective-permute-start = (f32[2,32,128]{2,1,0:T(8,128)S(1)}, f32[2,32,128]{2,1,0:T(8,128)S(1)}, u32[]{:S(2)}, u32[]{:S(2)}) collective-permute-start(f32[2,32,128]{2,1,0:T(8,128)S(1)} %get-tuple-element.13), channel_id=1, source_target_pairs={{0,8},{4,12},{8,0},{12,4},{1,9},{5,13},{9,1},{13,5},{2,10},{6,14},... | collective-permute-start | bytes 98312 | tf_op jit(solution)/shard_map/ppermute | solution.py:88
  7.0 7.9 %collective-permute-start.1 = (f32[2,32,128]{2,1,0:T(8,128)S(1)}, f32[2,32,128]{2,1,0:T(8,128)S(1)}, u32[]{:S(2)}, u32[]{:S(2)}) collective-permute-start(f32[2,32,128]{2,1,0:T(8,128)S(1)} %get-tuple-element.14), channel_id=1, source_target_pairs={{0,4},{4,8},{8,12},{12,0},{1,5},{5,9},{9,13},{13,1},{2,6},{6,10},{... | collective-permute-start | bytes 98312 | tf_op jit(solution)/shard_map/ppermute | solution.py:88
  8.5 6.3 %collective-permute-start.2 = (f32[2,32,128]{2,1,0:T(8,128)S(1)}, f32[2,32,128]{2,1,0:T(8,128)S(1)}, u32[]{:S(2)}, u32[]{:S(2)}) collective-permute-start(f32[2,32,128]{2,1,0:T(8,128)S(1)} %get-tuple-element.15), channel_id=1, source_target_pairs={{0,12},{4,0},{8,4},{12,8},{1,13},{5,1},{9,5},{13,9},{2,14},{6,2},{... | collective-permute-start | bytes 98312 | tf_op jit(solution)/shard_map/ppermute | solution.py:88
  10.8 8.4 %collective-permute-start.3 = (f16[11,32,128]{2,1,0:T(8,128)(2,1)S(1)}, f16[11,32,128]{2,1,0:T(8,128)(2,1)S(1)}, u32[]{:S(2)}, u32[]{:S(2)}) collective-permute-start(f16[11,32,128]{2,1,0:T(8,128)(2,1)S(1)} %convert_element_type.18), channel_id=1, source_target_pairs={{0,8},{4,12},{8,0},{12,4},{1,9},{5,13},{9,1},{13,5},{2,10},{6,14},... | collective-permute-start | bytes 270344 | tf_op jit(solution)/shard_map/ppermute | solution.py:88
  10.9 8.3 %collective-permute-start.4 = (f16[11,32,128]{2,1,0:T(8,128)(2,1)S(1)}, f16[11,32,128]{2,1,0:T(8,128)(2,1)S(1)}, u32[]{:S(2)}, u32[]{:S(2)}) collective-permute-start(f16[11,32,128]{2,1,0:T(8,128)(2,1)S(1)} %convert_element_type.20), channel_id=1, source_target_pairs={{0,4},{4,8},{8,12},{12,0},{1,5},{5,9},{9,13},{13,1},{2,6},{6,10},{... | collective-permute-start | bytes 270344 | tf_op jit(solution)/shard_map/ppermute | solution.py:88
  11.5 8.0 %collective-permute-start.5 = (f16[11,32,128]{2,1,0:T(8,128)(2,1)S(1)}, f16[11,32,128]{2,1,0:T(8,128)(2,1)S(1)}, u32[]{:S(2)}, u32[]{:S(2)}) collective-permute-start(f16[11,32,128]{2,1,0:T(8,128)(2,1)S(1)} %convert_element_type.22), channel_id=1, source_target_pairs={{0,12},{4,0},{8,4},{12,8},{1,13},{5,1},{9,5},{13,9},{2,14},{6,2},{... | collective-permute-start | bytes 270344 | tf_op jit(solution)/shard_map/ppermute | solution.py:88
  14.9 5.5 %copy-start.1 = (f32[1,32,128]{2,1,0:T(8,128)}, f32[1,32,128]{2,1,0:T(8,128)S(1)}, u32[]{:S(2)}) copy-start(f32[1,32,128]{2,1,0:T(8,128)S(1)} %get-tuple-element.21) | copy-start | bytes 49156
  15.0 3.7 %collective-permute-start.6 = (f32[32,5]{1,0:T(8,128)S(1)}, f32[32,5]{1,0:T(8,128)S(1)}, u32[]{:S(2)}, u32[]{:S(2)}) collective-permute-start(f32[32,5]{1,0:T(8,128)S(1)} %slice_select_fusion), channel_id=1, source_target_pairs={{0,2},{2,0},{1,3},{3,1},{4,6},{6,4},{5,7},{7,5},{8,10},{10,8},{9,1... | collective-permute-start | bytes 1928 | tf_op jit(solution)/shard_map/ppermute | solution.py:111
  19.6 0.8 %copy-start = (f32[11,32,128]{2,1,0:T(8,128)}, f32[11,32,128]{2,1,0:T(8,128)S(1)}, u32[]{:S(2)}) copy-start(f32[11,32,128]{2,1,0:T(8,128)S(1)} %add_divide_fusion) | copy-start | bytes 540676
